TPU v7x, 32 devices: a whole 2x2x4 slice. The times are simulated.
32 devices in a mesh: fsdp: 4 (over x, core), ctx: 8 (over z, y).
Axes of the slice: x: 2, y: 2, z: 4, core: 2. Of those that a mesh axis runs over, the one named last changes fastest.
Arguments:
- inputs: bfloat16 [4096, 1536], P(('fsdp', 'ctx')), may hold values from -6 to 6
- positions: int32 [4096], P(('fsdp', 'ctx')), may hold values from 0 to 1023, as said below
- cotangent: bfloat16 [4096, 1536], P(('fsdp', 'ctx')), may hold values from -6 to 6
- attention_gain: bfloat16 [1536], replicated, may hold values from 0.5 to 1.5
- query_weight: bfloat16 [1536, 1536], P('fsdp'), may hold values from -0.15625 to 0.15625
- key_weight: bfloat16 [768, 1536], P('fsdp'), may hold values from -0.15625 to 0.15625
- value_weight: bfloat16 [768, 1536], P('fsdp'), may hold values from -0.15625 to 0.15625
- output_weight: bfloat16 [1536, 1536], P('fsdp'), may hold values from -3 to 3
- feedforward_gain: bfloat16 [1536], replicated, may hold values from 0.5 to 1.5
- gate_weight: bfloat16 [4096, 1536], P('fsdp'), may hold values from -0.15625 to 0.15625
- up_weight: bfloat16 [4096, 1536], P('fsdp'), may hold values from -0.15625 to 0.15625
- down_weight: bfloat16 [4096, 1536], P('fsdp'), may hold values from -0.09375 to 0.09375
Outputs:
- layer_output: bfloat16 [4096, 1536], P(('fsdp', 'ctx'))
- input_grad: float32 [4096, 1536], P(('fsdp', 'ctx'))
- attention_gain_grad: float32 [1536], replicated
- query_weight_grad: float32 [1536, 1536], P('fsdp')
- key_weight_grad: float32 [768, 1536], P('fsdp')
- value_weight_grad: float32 [768, 1536], P('fsdp')
- output_weight_grad: float32 [1536, 1536], P('fsdp')
- feedforward_gain_grad: float32 [1536], replicated
- gate_weight_grad: float32 [4096, 1536], P('fsdp')
- up_weight_grad: float32 [4096, 1536], P('fsdp')
- down_weight_grad: float32 [4096, 1536], P('fsdp')
Inputs may be any that keep to these rules, and one draw needn't show every extreme that they name: Within each sequence every position appears once, and each device's 2 * 64 tokens of a sequence are two whole blocks of 64 consecutive rising positions, starting at b * 64 and at (15 - b) * 64 for some b, in either order.
All inputs are finite; a program needn't handle non-finite values.
Results may differ from a plain program's by a relative error of at most 0.022.
Values may be sent and summed in bfloat16 or wider, within the bound.
A program may use at most 384 MiB of HBM per device.

v0:
```python
import math
import jax
import jax.numpy as jnp
from jax import lax
from jax.sharding import PartitionSpec as P

HEADS = 16
KV_HEADS = 8
HEAD_DIM = 96
EPSILON = 1e-05
ROPE_BASE = 100000.0


def product(left, right):
    return jnp.dot(left, right, preferred_element_type=jnp.float32)


def product_back(left, right):
    return lax.dot_general(
        left, right, (((1,), (1,)), ((), ())), preferred_element_type=jnp.float32
    )


def product_rows(left, right):
    return lax.dot_general(
        left, right, (((0,), (0,)), ((), ())), preferred_element_type=jnp.float32
    )


def rms_scale(values):
    return lax.rsqrt(jnp.mean(values * values, axis=-1, keepdims=True) + EPSILON)


def norm_back(scale_rows, unit_rows, grad_unit):
    return scale_rows * (
        grad_unit - unit_rows * jnp.mean(grad_unit * unit_rows, axis=-1, keepdims=True)
    )


def rotary_tables(places):
    half_width = HEAD_DIM // 2
    frequencies = ROPE_BASE ** (-(jnp.arange(half_width, dtype=jnp.float32) * 2.0 / HEAD_DIM))
    angles = places.astype(jnp.float32)[:, None] * frequencies[None, :]
    return (jnp.cos(angles)[:, None, :], jnp.sin(angles)[:, None, :])


def rotate(values, cosine, sine):
    half_width = values.shape[-1] // 2
    lower_half = values[..., :half_width]
    upper_half = values[..., half_width:]
    return jnp.concatenate(
        [lower_half * cosine - upper_half * sine, upper_half * cosine + lower_half * sine], axis=-1
    )


def rotate_back(grads, cosine, sine):
    half_width = grads.shape[-1] // 2
    lower_half = grads[..., :half_width]
    upper_half = grads[..., half_width:]
    return jnp.concatenate(
        [lower_half * cosine + upper_half * sine, upper_half * cosine - lower_half * sine], axis=-1
    )


def block_total_of(total_keys):
    return max(1, total_keys // 512)


def masked_scores(query_grouped, query_places, key_rows, key_places, start, width):
    key_part = lax.dynamic_slice_in_dim(key_rows, start, width, 2)
    place_part = lax.dynamic_slice_in_dim(key_places, start, width, 1)
    scores = jnp.einsum(
        "sqhgd,shkd->shgqk", query_grouped, key_part, preferred_element_type=jnp.float32
    )
    scores = scores * (1.0 / math.sqrt(HEAD_DIM))
    allowed = place_part[:, None, None, None, :] <= query_places[:, None, None, :, None]
    return jnp.where(allowed, scores, -1000000000.0)


def attend_forward(query_grouped, query_places, key_rows, value_rows, key_places):
    seq_count, row_count, head_groups, group_size = query_grouped.shape[:4]
    total_keys = key_rows.shape[2]
    block_total = block_total_of(total_keys)
    width = total_keys // block_total
    stat_shape = (seq_count, head_groups, group_size, row_count)

    def peak_step(index, carry):
        running_top, running_sum = carry
        scores = masked_scores(
            query_grouped, query_places, key_rows, key_places, index * width, width
        )
        new_top = jnp.maximum(running_top, jnp.max(scores, axis=-1))
        running_sum = running_sum * jnp.exp(running_top - new_top) + jnp.sum(
            jnp.exp(scores - new_top[..., None]), axis=-1
        )
        return (new_top, running_sum)

    running_top, running_sum = lax.fori_loop(
        0,
        block_total,
        peak_step,
        (jnp.full(stat_shape, -1e30, jnp.float32), jnp.zeros(stat_shape, jnp.float32)),
    )
    log_total = running_top + jnp.log(running_sum)

    def value_step(index, gathered):
        scores = masked_scores(
            query_grouped, query_places, key_rows, key_places, index * width, width
        )
        soft_low = jnp.exp(scores - log_total[..., None]).astype(jnp.bfloat16)
        value_part = lax.dynamic_slice_in_dim(value_rows, index * width, width, 2)
        return gathered + jnp.einsum(
            "shgqk,shkd->sqhgd", soft_low, value_part, preferred_element_type=jnp.float32
        )

    attended = lax.fori_loop(
        0, block_total, value_step, jnp.zeros(query_grouped.shape, jnp.float32)
    )
    return (attended, log_total)


def attend_backward(
    query_grouped, query_places, key_rows, value_rows, key_places, log_total, grad_attended
):
    total_keys = key_rows.shape[2]
    block_total = block_total_of(total_keys)
    width = total_keys // block_total
    score_scale = 1.0 / math.sqrt(HEAD_DIM)

    def soft_and_grad(index):
        scores = masked_scores(
            query_grouped, query_places, key_rows, key_places, index * width, width
        )
        soft_values = jnp.exp(scores - log_total[..., None])
        value_part = lax.dynamic_slice_in_dim(value_rows, index * width, width, 2)
        grad_soft = jnp.einsum(
            "sqhgd,shkd->shgqk", grad_attended, value_part, preferred_element_type=jnp.float32
        )
        return (soft_values, grad_soft)

    def delta_step(index, row_delta):
        soft_values, grad_soft = soft_and_grad(index)
        return row_delta + jnp.sum(soft_values * grad_soft, axis=-1)

    row_delta = lax.fori_loop(0, block_total, delta_step, jnp.zeros(log_total.shape, jnp.float32))

    def grad_step(index, carry):
        grad_query, grad_keys, grad_values = carry
        soft_values, grad_soft = soft_and_grad(index)
        grad_scores = (soft_values * (grad_soft - row_delta[..., None])).astype(jnp.bfloat16)
        key_part = lax.dynamic_slice_in_dim(key_rows, index * width, width, 2)
        grad_query = (
            grad_query
            + jnp.einsum(
                "shgqk,shkd->sqhgd", grad_scores, key_part, preferred_element_type=jnp.float32
            )
            * score_scale
        )
        key_term = (
            jnp.einsum(
                "shgqk,sqhgd->shkd", grad_scores, query_grouped, preferred_element_type=jnp.float32
            )
            * score_scale
        )
        value_term = jnp.einsum(
            "shgqk,sqhgd->shkd",
            soft_values.astype(jnp.bfloat16),
            grad_attended,
            preferred_element_type=jnp.float32,
        )
        grad_keys = lax.dynamic_update_slice_in_dim(grad_keys, key_term, index * width, 2)
        grad_values = lax.dynamic_update_slice_in_dim(grad_values, value_term, index * width, 2)
        return (grad_query, grad_keys, grad_values)

    initial = (
        jnp.zeros(query_grouped.shape, jnp.float32),
        jnp.zeros(key_rows.shape, jnp.float32),
        jnp.zeros(value_rows.shape, jnp.float32),
    )
    return lax.fori_loop(0, block_total, grad_step, initial)


def gather_rows(values):
    return lax.all_gather(values, "fsdp", axis=0, tiled=True)


def scatter_rows(values):
    return lax.psum_scatter(
        values.astype(jnp.bfloat16), "fsdp", scatter_dimension=0, tiled=True
    ).astype(jnp.float32)


def per_device(
    inputs,
    positions,
    cotangent,
    attention_gain,
    query_weight,
    key_weight,
    value_weight,
    output_weight,
    feedforward_gain,
    gate_weight,
    up_weight,
    down_weight,
):
    row_count = inputs.shape[0]
    groups = HEADS // KV_HEADS
    gain_one = attention_gain.astype(jnp.float32)
    gain_two = feedforward_gain.astype(jnp.float32)
    seq_count = lax.axis_size("fsdp")
    first_row = lax.axis_index("fsdp") * row_count

    def own(values):
        return lax.dynamic_slice_in_dim(values, first_row, row_count, 0)

    query_places = gather_rows(positions).reshape(seq_count, row_count)
    key_places = lax.all_gather(query_places, "ctx", axis=1, tiled=True)
    all_cotangent = gather_rows(cotangent)
    flat_in = gather_rows(inputs).astype(jnp.float32)
    scale_one = rms_scale(flat_in)
    unit_one = flat_in * scale_one
    normed_one = (unit_one * gain_one).astype(jnp.bfloat16)
    total_rows = normed_one.shape[0]
    cosine, sine = rotary_tables(query_places.reshape(-1))
    query_heads = query_weight.shape[0] // HEAD_DIM
    kv_heads = key_weight.shape[0] // HEAD_DIM
    kv_width = kv_heads * HEAD_DIM
    query_low = rotate(
        product_back(normed_one, query_weight).reshape(total_rows, query_heads, HEAD_DIM),
        cosine,
        sine,
    ).astype(jnp.bfloat16)
    key_low = rotate(
        product_back(normed_one, key_weight).reshape(total_rows, kv_heads, HEAD_DIM), cosine, sine
    ).astype(jnp.bfloat16)
    value_low = product_back(normed_one, value_weight).astype(jnp.bfloat16)
    ctx_size = lax.axis_size("ctx")

    def spread(values):
        rows = lax.all_gather(values, "ctx", axis=0, tiled=True)
        rows = rows.reshape(ctx_size, seq_count, row_count, kv_width).swapaxes(0, 1)
        return rows.reshape(seq_count, ctx_size * row_count, kv_width)

    def collect(values):
        rows = values.astype(jnp.bfloat16).swapaxes(1, 2)
        rows = rows.reshape(seq_count, ctx_size, row_count, kv_width).swapaxes(0, 1)
        return lax.psum_scatter(rows.reshape(-1, kv_width), "ctx", scatter_dimension=0, tiled=True)

    all_keys = spread(key_low.reshape(total_rows, kv_width))
    all_values = spread(value_low)
    total_keys = all_keys.shape[1]
    key_grid = all_keys.reshape(seq_count, total_keys, kv_heads, HEAD_DIM).swapaxes(1, 2)
    value_grid = all_values.reshape(seq_count, total_keys, kv_heads, HEAD_DIM).swapaxes(1, 2)
    query_grouped = query_low.reshape(seq_count, row_count, kv_heads, groups, HEAD_DIM)
    attended, log_total = attend_forward(
        query_grouped, query_places, key_grid, value_grid, key_places
    )
    attended_low = attended.reshape(total_rows, query_heads * HEAD_DIM).astype(jnp.bfloat16)
    hidden_state = inputs.astype(jnp.float32) + scatter_rows(product(attended_low, output_weight))
    scale_two = rms_scale(hidden_state)
    unit_two = hidden_state * scale_two
    normed_two = gather_rows((unit_two * gain_two).astype(jnp.bfloat16))
    gate_values = product_back(normed_two, gate_weight)
    upward = product_back(normed_two, up_weight)
    sigmoid_gate = jax.nn.sigmoid(gate_values)
    activated = gate_values * sigmoid_gate
    mixed_hidden = (activated * upward).astype(jnp.bfloat16)
    grad_out = cotangent.astype(jnp.float32)
    grad_down = product_rows(mixed_hidden, all_cotangent)
    grad_mixed = product_back(all_cotangent, down_weight)
    grad_gate_low = (
        grad_mixed * upward * sigmoid_gate * (1.0 + gate_values * (1.0 - sigmoid_gate))
    ).astype(jnp.bfloat16)
    grad_up_low = (grad_mixed * activated).astype(jnp.bfloat16)
    grad_normed_two = scatter_rows(
        product(grad_gate_low, gate_weight) + product(grad_up_low, up_weight)
    )
    gain_two_grad = jnp.sum(grad_normed_two * unit_two, axis=0)
    grad_hidden = grad_out + norm_back(scale_two, unit_two, grad_normed_two * gain_two)
    branch_rows = gather_rows(grad_hidden.astype(jnp.bfloat16))
    layer_output = (hidden_state + scatter_rows(product(mixed_hidden, down_weight))).astype(
        jnp.bfloat16
    )
    grad_gate = product_rows(grad_gate_low, normed_two)
    grad_up = product_rows(grad_up_low, normed_two)
    grad_output = product_rows(attended_low, branch_rows)
    grad_attended = product_back(branch_rows, output_weight).astype(jnp.bfloat16)
    grad_attended = grad_attended.reshape(seq_count, row_count, kv_heads, groups, HEAD_DIM)
    grad_query_rot, grad_key_all, grad_value_all = attend_backward(
        query_grouped, query_places, key_grid, value_grid, key_places, log_total, grad_attended
    )
    grad_key_own = collect(grad_key_all).astype(jnp.float32)
    grad_value_low = collect(grad_value_all)
    grad_query_low = (
        rotate_back(grad_query_rot.reshape(total_rows, query_heads, HEAD_DIM), cosine, sine)
        .reshape(total_rows, query_heads * HEAD_DIM)
        .astype(jnp.bfloat16)
    )
    grad_key_low = (
        rotate_back(grad_key_own.reshape(total_rows, kv_heads, HEAD_DIM), cosine, sine)
        .reshape(total_rows, kv_width)
        .astype(jnp.bfloat16)
    )
    grad_query = product_rows(grad_query_low, normed_one)
    grad_key = product_rows(grad_key_low, normed_one)
    grad_value = product_rows(grad_value_low, normed_one)
    grad_normed_one = scatter_rows(
        product(grad_query_low, query_weight)
        + product(grad_key_low, key_weight)
        + product(grad_value_low, value_weight)
    )
    own_unit = own(unit_one)
    gain_one_grad = jnp.sum(grad_normed_one * own_unit, axis=0)
    input_grad = grad_hidden + norm_back(own(scale_one), own_unit, grad_normed_one * gain_one)

    def ctx_sum(grad):
        return lax.psum(grad.astype(jnp.bfloat16), "ctx").astype(jnp.float32)

    gain_sums = lax.psum(jnp.stack([gain_one_grad, gain_two_grad]), ("fsdp", "ctx"))
    return (
        layer_output,
        input_grad,
        gain_sums[0],
        ctx_sum(grad_query),
        ctx_sum(grad_key),
        ctx_sum(grad_value),
        ctx_sum(grad_output),
        gain_sums[1],
        ctx_sum(grad_gate),
        ctx_sum(grad_up),
        ctx_sum(grad_down),
    )


def solution(mesh):
    in_specs = (
        P(("fsdp", "ctx"), None),
        P(("fsdp", "ctx")),
        P(("fsdp", "ctx"), None),
        P(),
        P("fsdp", None),
        P("fsdp", None),
        P("fsdp", None),
        P("fsdp", None),
        P(),
        P("fsdp", None),
        P("fsdp", None),
        P("fsdp", None),
    )
    out_specs = (
        P(("fsdp", "ctx"), None),
        P(("fsdp", "ctx"), None),
        P(),
        P("fsdp", None),
        P("fsdp", None),
        P("fsdp", None),
        P("fsdp", None),
        P(),
        P("fsdp", None),
        P("fsdp", None),
        P("fsdp", None),
    )
    return jax.shard_map(
        per_device, mesh=mesh, in_specs=in_specs, out_specs=out_specs, check_vma=False
    )
```

profile of v0, /device:TPU:0, one launch (start us, length us, event | category | flops | bytes accessed | tf_op | source)
XLA Modules:
  0.0 985.5 jit_solution(4520594425977909812)
XLA Ops:
  8.8 6.2 all-gather
  15.5 16.5 %all-gather.8.cloned.1.call-done = bf16[512,1536]{1,0:T(8,128)(2,1)} async-done(((bf16[128,1536]{1,0:T(8,128)(2,1)}), bf16[512,1536]{1,0:T(8,128)(2,1)}) %all-gather.8.cloned.1.call-update) | async-done | bytes 1572880 | tf_op jit(solution)/shard_map/all_gather | solution.py:184
  36.9 26.4 %all_gather.27 = s32[4,1024]{1,0:T(4,128)S(1)} all-gather(s32[4,128]{1,0:T(4,128)S(1)} %bitcast.305), channel_id=1, replica_groups=mesh['fsdp'=4,'ctx'=8] {'ctx'}, dimensions={1}, use_global_device_ids=true | all-gather | bytes 18432 | tf_op jit(solution)/shard_map/all_gather | solution.py:218
  71.2 10.2 %all-gather.12.cloned.1.call-done = bf16[4096,192]{0,1:T(8,128)(2,1)} async-done(((bf16[512,192]{0,1:T(8,128)(2,1)}), bf16[4096,192]{0,1:T(8,128)(2,1)}) %all-gather.12.cloned.1.call-update) | async-done | bytes 1572880 | tf_op jit(solution)/shard_map/all_gather | solution.py:241
  81.4 3.8 reshape.215
  88.0 3.7 reshape_reshape.7
  91.7 20.6 %while.62 = (s32[]{:T(128)}, f32[4,2,2,128]{3,2,1,0:T(2,128)}, f32[4,2,2,128]{3,2,1,0:T(2,128)}, s32[4,1024]{1,0:T(4,128)S(1)}, s32[512]{0:T(512)}, /*index=5*/b...) while((s32[]{:T(128)}, f32[4,2,2,128]{3,2,1,0:T(2,128)}, ...), condition=%wide.region_4.5_spmd.clone, body=%wide.region_1.4_spmd.clone.sunk | while | flops 208939008 | bytes 11634982 | solution.py:98
  92.8 4.7 fusion.162
  103.0 4.7 fusion.162
  108.5 3.2 exponential_reduce_fusion.2
  112.3 14.3 %all-gather.10.cloned.1.call-done = bf16[4096,192]{0,1:T(8,128)(2,1)} async-done(((bf16[512,192]{0,1:T(8,128)(2,1)}), bf16[4096,192]{0,1:T(8,128)(2,1)}) %all-gather.10.cloned.1.call-update) | async-done | bytes 1572880 | tf_op jit(solution)/shard_map/all_gather | solution.py:241
  126.6 3.8 reshape.212
  133.2 3.7 reshape_reshape.6
  138.2 11.5 %while.63 = (s32[]{:T(128)}, f32[4,128,2,2,96]{1,4,3,2,0:T(8,128)}, bf16[4,2,1024,96]{2,3,1,0:T(8,128)(2,1)}, s32[4,1024]{1,0:T(4,128)S(1)}, s32[512]{0:T(512)},...) while((s32[]{:T(128)}, f32[4,128,2,2,96]{1,4,3,2,0:T(8,128)}, ...), condition=%wide.region_6.7_spmd.clone, body=%wide.region_5.6_spmd.clone.sunk | while | flops 407502848 | bytes 4099768 | solution.py:116
  139.9 3.9 fusion.168
  145.5 4.1 fusion.168
  151.9 3.4 convolution_convert_fusion.4
  156.7 25.1 %reduce-scatter.7.cloned.1.call-done = bf16[128,1536]{1,0:T(8,128)(2,1)} async-done(((bf16[512,1536]{1,0:T(8,128)(2,1)}), bf16[128,1536]{1,0:T(8,128)(2,1)}) %reduce-scatter.7.cloned.1.call-update) | async-done | bytes 393232 | tf_op jit(solution)/shard_map/reduce_scatter | solution.py:188
  186.5 19.0 %all-gather.14.cloned.1.call-done = bf16[512,1536]{1,0:T(8,128)(2,1)} async-done(((bf16[128,1536]{1,0:T(8,128)(2,1)}), bf16[512,1536]{1,0:T(8,128)(2,1)}) %all-gather.14.cloned.1.call-update) | async-done | bytes 1572880 | tf_op jit(solution)/shard_map/all_gather | solution.py:184
  205.5 5.6 fusion.85
  214.3 12.3 %all-gather.16.cloned.1.call-done = bf16[512,1536]{1,0:T(8,128)(2,1)} async-done(((bf16[128,1536]{1,0:T(8,128)(2,1)}), bf16[512,1536]{1,0:T(8,128)(2,1)}) %all-gather.16.cloned.1.call-update) | async-done | bytes 1572880 | tf_op jit(solution)/shard_map/all_gather | solution.py:184
  226.6 6.3 multiply_convert_fusion.1
  238.6 28.1 %reduce-scatter.11.cloned.1.call-done = bf16[128,1536]{1,0:T(8,128)(2,1)} async-done(((bf16[512,1536]{1,0:T(8,128)(2,1)}), bf16[128,1536]{1,0:T(8,128)(2,1)}) %reduce-scatter.11.cloned.1.call-update) | async-done | bytes 393232 | tf_op jit(solution)/shard_map/reduce_scatter | solution.py:188
  272.2 19.5 %all-gather.18.cloned.1.call-done = bf16[512,1536]{1,0:T(8,128)(2,1)} async-done(((bf16[128,1536]{1,0:T(8,128)(2,1)}), bf16[512,1536]{1,0:T(8,128)(2,1)}) %all-gather.18.cloned.1.call-update) | async-done | bytes 1572880 | tf_op jit(solution)/shard_map/all_gather | solution.py:184
  291.7 3.5 convolution_convert_fusion.9
  299.2 11.5 %while.64 = (s32[]{:T(128)}, f32[4,2,2,128]{3,2,1,0:T(2,128)}, s32[4,1024]{1,0:T(4,128)S(1)}, s32[512]{0:T(512)}, bf16[4,2,1024,96]{2,3,1,0:T(8,128)(2,1)}, /*in...) while((s32[]{:T(128)}, f32[4,2,2,128]{3,2,1,0:T(2,128)}, ...), condition=%wide.region_14.0_spmd.clone, body=%wide.region_12.0_spmd.clone.sunk | while | flops 408160256 | bytes 19245368 | solution.py:145
  313.5 29.0 %while.65 = (s32[]{:T(128)}, f32[4,128,2,2,96]{1,4,3,2,0:T(8,128)}, bf16[4,2,1024,96]{2,3,1,0:T(8,128)(2,1)}, bf16[4,2,1024,96]{2,3,1,0:T(8,128)(2,1)}, bf16[4,2...) while((s32[]{:T(128)}, f32[4,128,2,2,96]{1,4,3,2,0:T(8,128)}, ...), condition=%wide.region_16.17_spmd.clone, body=%wide.region_15.16_spmd.clone.sunk | while | flops 1018363904 | bytes 86141536 | solution.py:180
  318.8 3.4 fusion.187
  322.2 3.4 fusion.188
  333.2 3.5 fusion.187
  336.8 3.4 fusion.188
  344.3 3.2 copy.110
  347.5 3.8 reshape.220
  356.9 3.8 reshape.224
  369.8 47.8 %reduce-scatter.13.cloned.1.call-done = bf16[512,192]{0,1:T(8,128)(2,1)} async-done(((bf16[4096,192]{0,1:T(8,128)(2,1)}), bf16[512,192]{0,1:T(8,128)(2,1)}) %reduce-scatter.13.cloned.1.call-update) | async-done | bytes 196624 | tf_op jit(solution)/shard_map/reduce_scatter | solution.py:248
  420.4 4.2 convolution_add_fusion.1
  424.6 62.0 %reduce-scatter.15.cloned.1.call-done = bf16[512,192]{0,1:T(8,128)(2,1)} async-done(((bf16[4096,192]{0,1:T(8,128)(2,1)}), bf16[512,192]{0,1:T(8,128)(2,1)}) %reduce-scatter.15.cloned.1.call-update) | async-done | bytes 196624 | tf_op jit(solution)/shard_map/reduce_scatter | solution.py:248
  486.6 3.9 fusion.63
  490.5 4.2 convolution_convert_fusion.3
  495.0 5.5 convolution_convert_fusion.2
  500.5 3.5 convolution_convert_fusion.1
  504.1 3.5 convolution_convert_fusion
  514.9 3.4 convert_multiply_fusion
  522.3 39.8 %psum.56 = f32[2,1536]{1,0:T(2,128)} all-reduce(f32[2,1536]{1,0:T(2,128)} %pad_maximum_fusion.4), channel_id=1, replica_groups=mesh['fsdp'=4,'ctx'=8] {'fsdp','ctx'}, use_global_device_ids=true, to_apply=%region_23.24 | all-reduce | flops 3072 | bytes 24576 | tf_op jit(solution)/shard_map/psum | solution.py:320
  567.8 392.1 %all-reduce.3.cloned.1.call-done = (bf16[384,1536]{1,0:T(8,128)(2,1)}, bf16[192,1536]{1,0:T(8,128)(2,1)}, bf16[192,1536]{1,0:T(8,128)(2,1)}, bf16[384,1536]{1,0:...) async-done(((bf16[384,1536]{1,0:T(8,128)(2,1)}, bf16[192,1536]{1,0:T(8,128)(2,1)}, bf16[192,1536]{1,0:T(8,128)(2,1)}, ...) | async-done | bytes 12976144 | tf_op jit(solution)/shard_map/psum | solution.py:318
  968.0 3.6 convert_element_type.199
  971.6 3.6 convert_element_type.201
  975.2 3.6 convert_element_type.203
  (294 shorter events, 133.4 us)
Async XLA Ops:
  7.2 219.5 %copy-start = (bf16[1024,1536]{1,0:T(8,128)(2,1)S(1)}, bf16[1024,1536]{1,0:T(8,128)(2,1)}, u32[]{:S(2)}) copy-start(bf16[1024,1536]{1,0:T(8,128)(2,1)} %param.31) | copy-start | bytes 9437188
  7.2 24.8 %all-gather.8.cloned.1.call-start = ((), (), s32[]{:S(2)}) async-start(), calls=%async_computation.6 | async-start | bytes 1966080 | tf_op jit(solution)/shard_map/all_gather | solution.py:184
  7.9 73.5 %all-gather.12.cloned.1.call-start = ((), (), s32[]{:S(2)}) async-start(), calls=%async_computation.8 | async-start | bytes 1769472 | tf_op jit(solution)/shard_map/all_gather | solution.py:241
  8.8 54.5 %copy-start.40 = (f32[1536]{0:T(1024)}, f32[1536]{0:T(1024)S(1)}, u32[]{:S(2)}) copy-start(f32[1536]{0:T(1024)S(1)} %convert_element_type.162) | copy-start | bytes 18436
  15.0 21.9 %copy-start.23 = (s32[4,1,128]{2,1,0:T(1,128)}, s32[4,1,128]{2,1,0:T(1,128)S(1)}, u32[]{:S(2)}) copy-start(s32[4,1,128]{2,1,0:T(1,128)S(1)} %all-gather) | copy-start | bytes 6148
  15.5 50.5 %copy-start.13 = (f32[512,48]{0,1:T(8,128)}, f32[512,48]{0,1:T(8,128)S(1)}, u32[]{:S(2)}) copy-start(f32[512,48]{0,1:T(8,128)S(1)} %get-tuple-element.994) | copy-start | bytes 294916
  15.5 50.5 %copy-start.15 = (f32[512,48]{0,1:T(8,128)}, f32[512,48]{0,1:T(8,128)S(1)}, u32[]{:S(2)}) copy-start(f32[512,48]{0,1:T(8,128)S(1)} %get-tuple-element.995) | copy-start | bytes 294916
  33.7 29.5 %copy-start.44 = (f32[512]{0:T(512)}, f32[512]{0:T(512)S(1)}, u32[]{:S(2)}) copy-start(f32[512]{0:T(512)S(1)} %add_rsqrt_fusion) | copy-start | bytes 6148
  36.8 89.8 %all-gather.10.cloned.1.call-start = ((), (), s32[]{:S(2)}) async-start(), calls=%async_computation.7 | async-start | bytes 1769472 | tf_op jit(solution)/shard_map/all_gather | solution.py:241
  71.2 110.6 %reduce-scatter.7.cloned.1.call-start = ((), (), s32[]{:S(2)}) async-start(), calls=%async_computation.9 | async-start | bytes 1966080 | tf_op jit(solution)/shard_map/reduce_scatter | solution.py:188
  92.8 4.7 copy-start.3
  103.0 4.7 copy-start.3
  155.4 50.1 %all-gather.14.cloned.1.call-start = ((), (), s32[]{:S(2)}) async-start(), calls=%async_computation.10 | async-start | bytes 1966080 | tf_op jit(solution)/shard_map/all_gather | solution.py:184
  185.7 40.9 %all-gather.16.cloned.1.call-start = ((), (), s32[]{:S(2)}) async-start(), calls=%async_computation.12 | async-start | bytes 1966080 | tf_op jit(solution)/shard_map/all_gather | solution.py:184
  186.3 80.4 %reduce-scatter.11.cloned.1.call-start = ((), (), s32[]{:S(2)}) async-start(), calls=%async_computation.13 | async-start | bytes 1966080 | tf_op jit(solution)/shard_map/reduce_scatter | solution.py:188
  205.5 5.7 copy-start.51
  205.5 5.7 copy-start.53
  226.6 6.3 copy-start.50
  238.6 53.1 %all-gather.18.cloned.1.call-start = ((), (), s32[]{:S(2)}) async-start(), calls=%async_computation.14 | async-start | bytes 1966080 | tf_op jit(solution)/shard_map/all_gather | solution.py:184
  271.9 145.8 %reduce-scatter.13.cloned.1.call-start = ((), (), s32[]{:S(2)}) async-start(), calls=%async_computation.15 | async-start | bytes 1769472 | tf_op jit(solution)/shard_map/reduce_scatter | solution.py:248
  318.8 6.8 copy-start.2
  322.1 3.4 copy-start.6
  322.1 3.4 copy-start.7
  322.1 3.4 copy-start.34
  322.1 3.4 copy-start.48
  333.2 6.9 copy-start.2
  336.7 3.4 copy-start.6
  336.7 3.4 copy-start.7
  336.8 3.4 copy-start.34
  336.8 3.4 copy-start.48
  351.4 135.2 %reduce-scatter.15.cloned.1.call-start = ((), (), s32[]{:S(2)}) async-start(), calls=%async_computation.16 | async-start | bytes 1769472 | tf_op jit(solution)/shard_map/reduce_scatter | solution.py:248
  360.7 5.0 copy-start.14
  360.7 5.0 copy-start.16
  360.7 158.2 %reduce-scatter.17.cloned.1.call-start = ((), (), s32[]{:S(2)}) async-start(), calls=%async_computation.17 | async-start | bytes 1966080 | tf_op jit(solution)/shard_map/reduce_scatter | solution.py:188
  490.5 74.2 %reduce-scatter.9.cloned.1.call-start = ((), (), s32[]{:S(2)}) async-start(), calls=%async_computation.11 | async-start | bytes 1966080 | tf_op jit(solution)/shard_map/reduce_scatter | solution.py:188
  494.7 465.2 %all-reduce.3.cloned.1.call-start = ((), (), s32[]{:S(2)}) async-start(), calls=%async_computation.18 | async-start | bytes 25952256 | tf_op jit(solution)/shard_map/psum | solution.py:318
  495.0 5.6 copy-start.54
  495.0 5.6 copy-start.58
  500.5 3.5 copy-start.55
  500.5 3.5 copy-start.60
  504.1 3.5 copy-start.20
  504.1 3.5 copy-start.56
  514.9 3.4 copy-start.42
  514.9 49.8 %copy-start.4 = (bf16[128,1536]{1,0:T(8,128)(2,1)S(1)}, bf16[128,1536]{1,0:T(8,128)(2,1)}, u32[]{:S(2)}) copy-start(bf16[128,1536]{1,0:T(8,128)(2,1)} %param.20) | copy-start | bytes 1179652
  514.9 49.8 %copy-start.37 = (f32[1536]{0:T(1024)S(1)}, f32[1536]{0:T(1024)}, u32[]{:S(2)}) copy-start(f32[1536]{0:T(1024)} %convert_element_type.171) | copy-start | bytes 18436
  959.9 4.2 copy-start.30
  968.0 3.6 copy-start.11
  971.6 3.6 copy-start.10
  (47 other events, 101.3 us)
Sparse Core Ops, SparseCore 0:
  9.6 22.3 all-gather.7
  37.0 44.4 all-gather.11
  84.1 42.5 all-gather.9
  155.5 26.2 reduce-scatter.6
  185.8 19.6 all-gather.13
  206.9 19.6 all-gather.15
  238.7 27.9 reduce-scatter.10
  272.0 19.6 all-gather.17
  351.5 66.1 reduce-scatter.12
  421.5 65.0 reduce-scatter.14
  490.6 26.7 reduce-scatter.16
  520.4 27.9 reduce-scatter.8
  555.3 404.5 all-reduce.2
where the time goes:
time: 996 us; the launch traced here: 985 us
  waiting for transfers between devices  648 us (65%)
  matrix products  120 us (12%)
  blocking collectives  72.3 us (7%)
  other arithmetic  66.2 us (7%)
  local copies, waits for them, and re-layouts  62.1 us (6%)
  between operations  14.5 us (1%)
    psum x1, waiting for transfers between devices, ctx_sum(): return lax.psum(grad.astype(jnp.bfloat16), 'ctx').astype(jnp.float32)  392 us
    reduce_scatter x2, waiting for transfers between devices, collect(): lax.psum_scatter(rows.reshape(-1, kv_width), 'ctx', scatter_dimension=0,...  110 us
    all_gather x4, waiting for transfers between devices, gather_rows(): return lax.all_gather(values, 'fsdp', axis=0, tiled=True)  67.3 us
    reduce_scatter x4, waiting for transfers between devices, scatter_rows(): lax.psum_scatter(values.astype(jnp.bfloat16), 'fsdp', scatter_dimension=0...  53.2 us
    psum x1, blocking collectives, per_device(): lax.psum(jnp.stack([gain_one_grad, gain_two_grad]), ('fsdp', 'ctx'))  39.8 us
    dot_general x7, matrix products, product_back(): lax.dot_general(left, right, (((1,), (1,)), ((), ())), preferred_element_...  26.5 us
    all_gather x1, blocking collectives, per_device(): key_places = lax.all_gather(query_places, 'ctx', axis=1, tiled=True)  26.4 us
    all_gather x2, waiting for transfers between devices, spread(): rows = lax.all_gather(values, 'ctx', axis=0, tiled=True)  24.5 us
  transfers between devices with their start and end apart: 13, of which 11 were waited for; matrix products, arithmetic and copies ran while one was open for 11% of the time, Pallas kernels for 0%

commit v1 on v0

--- a/solution.py
+++ b/solution.py
@@ -238,7 +238,25 @@
     ctx_size = lax.axis_size("ctx")
 
     def spread(values):
-        rows = lax.all_gather(values, "ctx", axis=0, tiled=True)
+        w1 = lax.axis_size("ctx")
+        answer = lax.axis_index("ctx")
+        fresh, step_out, top = (w1, answer, values.shape[0])
+        cards = [(hop_no, (hop_no + 1) % fresh) for hop_no in range(fresh)]
+        table = [(hop_no, (hop_no - 1) % fresh) for hop_no in range(fresh)]
+        rows = jnp.zeros((*values.shape[:0], fresh * top, *values.shape[0 + 1 :]), values.dtype)
+        rows = lax.dynamic_update_slice_in_dim(rows, values, step_out * top, axis=0)
+        seen_now = fresh // 2
+        passed = kept_arr = values
+        for kk in range(1, seen_now + 1):
+            passed = lax.ppermute(passed, "ctx", cards)
+            rows = lax.dynamic_update_slice_in_dim(
+                rows, passed, (step_out - kk) % fresh * top, axis=0
+            )
+            if kk < fresh - seen_now:
+                kept_arr = lax.ppermute(kept_arr, "ctx", table)
+                rows = lax.dynamic_update_slice_in_dim(
+                    rows, kept_arr, (step_out + kk) % fresh * top, axis=0
+                )
         rows = rows.reshape(ctx_size, seq_count, row_count, kv_width).swapaxes(0, 1)
         return rows.reshape(seq_count, ctx_size * row_count, kv_width)
 

time: 996 us -> 1010 us (1.014)
  waiting for transfers between devices: 648 us -> 613 us
  starting transfers between devices: 1.49 us -> 35.7 us
  local copies, waits for them, and re-layouts: 62.1 us -> 79.2 us
    ppermute x0 -> x14, starting transfers between devices: none -> 34.2 us  [the longest x6 25 us: spread(): kept_arr = lax.ppermute(kept_arr, 'ctx', table)]
    all_gather x2 -> x0, waiting for transfers between devices: 24.5 us -> none  [spread(): rows = lax.all_gather(values, 'ctx', axis=0, tiled=True)]
    all_gather x4, waiting for transfers between devices: 67.3 us -> 50.8 us  [gather_rows(): return lax.all_gather(values, 'fsdp', axis=0, tiled=True)]
    dynamic_update_slice x0 -> x14, local copies, waits for them, and re-layouts: none -> 14.4 us  [the longest x7 6.75 us: spread(): lax.dynamic_update_slice_in_dim(rows, passed, (step_out - kk) % fresh * t...]
  transfers between devices with their start and end apart: 13 -> 25, of which waited for: 11 -> 12; matrix products, arithmetic and copies ran while one was open for 11% -> 9% of each run, Pallas kernels for 0% -> 0%
where the time goes in v1:
time: 1010 us; the launch traced here: 999 us
  waiting for transfers between devices  613 us (61%)
  matrix products  117 us (12%)
  local copies, waits for them, and re-layouts  79.2 us (8%)
  blocking collectives  72.9 us (7%)
  other arithmetic  66 us (7%)
  starting transfers between devices  35.7 us (4%)
  between operations  14.6 us (1%)
    psum x1, waiting for transfers between devices, ctx_sum(): return lax.psum(grad.astype(jnp.bfloat16), 'ctx').astype(jnp.float32)  392 us
    reduce_scatter x2, waiting for transfers between devices, collect(): lax.psum_scatter(rows.reshape(-1, kv_width), 'ctx', scatter_dimension=0,...  110 us
    reduce_scatter x4, waiting for transfers between devices, scatter_rows(): lax.psum_scatter(values.astype(jnp.bfloat16), 'fsdp', scatter_dimension=0...  53.7 us
    all_gather x4, waiting for transfers between devices, gather_rows(): return lax.all_gather(values, 'fsdp', axis=0, tiled=True)  50.8 us
    psum x1, blocking collectives, per_device(): lax.psum(jnp.stack([gain_one_grad, gain_two_grad]), ('fsdp', 'ctx'))  39.8 us
    all_gather x1, blocking collectives, per_device(): key_places = lax.all_gather(query_places, 'ctx', axis=1, tiled=True)  26.9 us
    ppermute x6, starting transfers between devices, spread(): kept_arr = lax.ppermute(kept_arr, 'ctx', table)  25 us
    dot_general x7, matrix products, product_back(): lax.dot_general(left, right, (((1,), (1,)), ((), ())), preferred_element_...  23.2 us
  transfers between devices with their start and end apart: 25, of which 12 were waited for; matrix products, arithmetic and copies ran while one was open for 9% of the time, Pallas kernels for 0%

profile of v1, /device:TPU:0, one launch (start us, length us, event | category | flops | bytes accessed | tf_op | source)
XLA Modules:
  0.0 999.0 jit_solution(17784719770986476142)
XLA Ops:
  8.8 6.2 all-gather
  15.0 26.9 %all_gather.20 = s32[4,1024]{1,0:T(4,128)S(1)} all-gather(s32[4,128]{1,0:T(4,128)S(1)} %bitcast.305), channel_id=1, replica_groups=mesh['fsdp'=4,'ctx'=8] {'ctx'}, dimensions={1}, use_global_device_ids=true | all-gather | bytes 18432 | tf_op jit(solution)/shard_map/all_gather | solution.py:218
  48.9 3.2 collective-permute-start.8
  54.9 4.7 collective-permute-start.1
  65.7 4.7 collective-permute-start.10
  73.7 4.7 collective-permute-start.3
  81.6 4.7 collective-permute-start.12
  108.8 3.8 reshape.215
  115.4 3.7 reshape_reshape.7
  119.1 20.5 %while.62 = (s32[]{:T(128)}, f32[4,2,2,128]{3,2,1,0:T(2,128)}, f32[4,2,2,128]{3,2,1,0:T(2,128)}, s32[4,1024]{1,0:T(4,128)S(1)}, s32[512]{0:T(512)}, /*index=5*/b...) while((s32[]{:T(128)}, f32[4,2,2,128]{3,2,1,0:T(2,128)}, ...), condition=%wide.region_4.5_spmd.clone, body=%wide.region_1.4_spmd.clone.sunk | while | flops 208939008 | bytes 11634982 | solution.py:98
  120.1 4.7 fusion.162
  130.3 4.7 fusion.162
  139.6 3.8 reshape.212
  146.1 3.7 reshape_reshape.6
  151.1 11.4 %while.63 = (s32[]{:T(128)}, f32[4,128,2,2,96]{1,4,3,2,0:T(8,128)}, bf16[4,2,1024,96]{2,3,1,0:T(8,128)(2,1)}, s32[4,1024]{1,0:T(4,128)S(1)}, s32[512]{0:T(512)},...) while((s32[]{:T(128)}, f32[4,128,2,2,96]{1,4,3,2,0:T(8,128)}, ...), condition=%wide.region_6.7_spmd.clone, body=%wide.region_5.6_spmd.clone.sunk | while | flops 407502848 | bytes 4099768 | solution.py:116
  152.8 3.9 fusion.168
  158.4 4.1 fusion.168
  164.8 3.4 convolution_convert_fusion.4
  169.6 25.6 %reduce-scatter.7.cloned.1.call-done = bf16[128,1536]{1,0:T(8,128)(2,1)} async-done(((bf16[512,1536]{1,0:T(8,128)(2,1)}), bf16[128,1536]{1,0:T(8,128)(2,1)}) %reduce-scatter.7.cloned.1.call-update) | async-done | bytes 393232 | tf_op jit(solution)/shard_map/reduce_scatter | solution.py:188
  199.9 19.0 %all-gather.8.cloned.1.call-done = bf16[512,1536]{1,0:T(8,128)(2,1)} async-done(((bf16[128,1536]{1,0:T(8,128)(2,1)}), bf16[512,1536]{1,0:T(8,128)(2,1)}) %all-gather.8.cloned.1.call-update) | async-done | bytes 1572880 | tf_op jit(solution)/shard_map/all_gather | solution.py:184
  218.9 5.6 fusion.85
  227.7 12.3 %all-gather.10.cloned.1.call-done = bf16[512,1536]{1,0:T(8,128)(2,1)} async-done(((bf16[128,1536]{1,0:T(8,128)(2,1)}), bf16[512,1536]{1,0:T(8,128)(2,1)}) %all-gather.10.cloned.1.call-update) | async-done | bytes 1572880 | tf_op jit(solution)/shard_map/all_gather | solution.py:184
  240.1 6.3 multiply_convert_fusion.1
  252.0 28.1 %reduce-scatter.11.cloned.1.call-done = bf16[128,1536]{1,0:T(8,128)(2,1)} async-done(((bf16[512,1536]{1,0:T(8,128)(2,1)}), bf16[128,1536]{1,0:T(8,128)(2,1)}) %reduce-scatter.11.cloned.1.call-update) | async-done | bytes 393232 | tf_op jit(solution)/shard_map/reduce_scatter | solution.py:188
  285.6 19.5 %all-gather.12.cloned.1.call-done = bf16[512,1536]{1,0:T(8,128)(2,1)} async-done(((bf16[128,1536]{1,0:T(8,128)(2,1)}), bf16[512,1536]{1,0:T(8,128)(2,1)}) %all-gather.12.cloned.1.call-update) | async-done | bytes 1572880 | tf_op jit(solution)/shard_map/all_gather | solution.py:184
  305.2 3.5 convolution_convert_fusion.9
  312.7 11.5 %while.64 = (s32[]{:T(128)}, f32[4,2,2,128]{3,2,1,0:T(2,128)}, s32[4,1024]{1,0:T(4,128)S(1)}, s32[512]{0:T(512)}, bf16[4,2,1024,96]{2,3,1,0:T(8,128)(2,1)}, /*in...) while((s32[]{:T(128)}, f32[4,2,2,128]{3,2,1,0:T(2,128)}, ...), condition=%wide.region_14.15_spmd.clone, body=%wide.region_12.14_spmd.clone.sunk | while | flops 408160256 | bytes 19245368 | solution.py:145
  326.9 29.0 %while.65 = (s32[]{:T(128)}, f32[4,128,2,2,96]{1,4,3,2,0:T(8,128)}, bf16[4,2,1024,96]{2,3,1,0:T(8,128)(2,1)}, bf16[4,2,1024,96]{2,3,1,0:T(8,128)(2,1)}, bf16[4,2...) while((s32[]{:T(128)}, f32[4,128,2,2,96]{1,4,3,2,0:T(8,128)}, ...), condition=%wide.region_16.17_spmd.clone, body=%wide.region_15.16_spmd.clone.sunk | while | flops 1018363904 | bytes 86141536 | solution.py:180
  332.3 3.4 fusion.187
  335.6 3.4 fusion.188
  346.7 3.5 fusion.187
  350.2 3.4 fusion.188
  361.0 3.8 reshape.220
  370.3 3.8 reshape.224
  383.3 47.8 %reduce-scatter.13.cloned.1.call-done = bf16[512,192]{0,1:T(8,128)(2,1)} async-done(((bf16[4096,192]{0,1:T(8,128)(2,1)}), bf16[512,192]{0,1:T(8,128)(2,1)}) %reduce-scatter.13.cloned.1.call-update) | async-done | bytes 196624 | tf_op jit(solution)/shard_map/reduce_scatter | solution.py:266
  433.8 4.2 convolution_add_fusion.1
  438.0 62.1 %reduce-scatter.15.cloned.1.call-done = bf16[512,192]{0,1:T(8,128)(2,1)} async-done(((bf16[4096,192]{0,1:T(8,128)(2,1)}), bf16[512,192]{0,1:T(8,128)(2,1)}) %reduce-scatter.15.cloned.1.call-update) | async-done | bytes 196624 | tf_op jit(solution)/shard_map/reduce_scatter | solution.py:266
  500.1 3.9 fusion.63
  504.1 4.2 convolution_convert_fusion.3
  508.5 5.5 convolution_convert_fusion.2
  514.0 3.5 convolution_convert_fusion.1
  517.6 3.5 convolution_convert_fusion
  528.5 3.4 convert_multiply_fusion
  535.8 39.8 %psum.56 = f32[2,1536]{1,0:T(2,128)} all-reduce(f32[2,1536]{1,0:T(2,128)} %pad_maximum_fusion.4), channel_id=1, replica_groups=mesh['fsdp'=4,'ctx'=8] {'fsdp','ctx'}, use_global_device_ids=true, to_apply=%region_23.24 | all-reduce | flops 3072 | bytes 24576 | tf_op jit(solution)/shard_map/psum | solution.py:338
  581.4 392.1 %all-reduce.3.cloned.1.call-done = (bf16[384,1536]{1,0:T(8,128)(2,1)}, bf16[192,1536]{1,0:T(8,128)(2,1)}, bf16[192,1536]{1,0:T(8,128)(2,1)}, bf16[384,1536]{1,0:...) async-done(((bf16[384,1536]{1,0:T(8,128)(2,1)}, bf16[192,1536]{1,0:T(8,128)(2,1)}, bf16[192,1536]{1,0:T(8,128)(2,1)}, ...) | async-done | bytes 12976144 | tf_op jit(solution)/shard_map/psum | solution.py:336
  981.6 3.6 convert_element_type.199
  985.1 3.6 convert_element_type.201
  988.7 3.6 convert_element_type.203
  (340 shorter events, 171.0 us)
Async XLA Ops:
  7.2 232.9 %copy-start = (bf16[1024,1536]{1,0:T(8,128)(2,1)S(1)}, bf16[1024,1536]{1,0:T(8,128)(2,1)}, u32[]{:S(2)}) copy-start(bf16[1024,1536]{1,0:T(8,128)(2,1)} %param.31) | copy-start | bytes 9437188
  7.2 35.2 %all-gather.6.cloned.1.call-start = ((), (), s32[]{:S(2)}) async-start(), calls=%async_computation.6 | async-start | bytes 1966080 | tf_op jit(solution)/shard_map/all_gather | solution.py:184
  7.9 187.2 %reduce-scatter.7.cloned.1.call-start = ((), (), s32[]{:S(2)}) async-start(), calls=%async_computation.7 | async-start | bytes 1966080 | tf_op jit(solution)/shard_map/reduce_scatter | solution.py:188
  8.8 37.7 %copy-start.43 = (f32[1536]{0:T(1024)}, f32[1536]{0:T(1024)S(1)}, u32[]{:S(2)}) copy-start(f32[1536]{0:T(1024)S(1)} %convert_element_type.162) | copy-start | bytes 18436
  15.0 26.9 %copy-start.25 = (s32[4,1,128]{2,1,0:T(1,128)}, s32[4,1,128]{2,1,0:T(1,128)S(1)}, u32[]{:S(2)}) copy-start(s32[4,1,128]{2,1,0:T(1,128)S(1)} %all-gather) | copy-start | bytes 6148
  42.4 18.2 %copy-start.14 = (f32[512,48]{0,1:T(8,128)}, f32[512,48]{0,1:T(8,128)S(1)}, u32[]{:S(2)}) copy-start(f32[512,48]{0,1:T(8,128)S(1)} %get-tuple-element.994) | copy-start | bytes 294916
  42.4 18.2 %copy-start.16 = (f32[512,48]{0,1:T(8,128)}, f32[512,48]{0,1:T(8,128)S(1)}, u32[]{:S(2)}) copy-start(f32[512,48]{0,1:T(8,128)S(1)} %get-tuple-element.995) | copy-start | bytes 294916
  44.3 15.4 %copy-start.48 = (f32[512]{0:T(512)}, f32[512]{0:T(512)S(1)}, u32[]{:S(2)}) copy-start(f32[512]{0:T(512)S(1)} %add_rsqrt_fusion) | copy-start | bytes 6148
  46.6 6.8 copy-start.9
  46.6 6.8 copy-start.34
  46.6 6.8 copy-start.44
  47.4 18.3 %collective-permute-start.7 = (bf16[512,192]{0,1:T(8,128)(2,1)}, bf16[512,192]{0,1:T(8,128)(2,1)}, u32[]{:S(2)}, u32[]{:S(2)}) collective-permute-start(bf16[512,192]{0,1:T(8,128)(2,1)} %bitcast.6), channel_id=1, source_target_pairs={{0,1},{1,2},{2,3},{3,4},{4,5},{5,6},{6,7},{7,0},{8,9},{9,10},{10,1... | collective-permute-start | bytes 589832 | tf_op jit(solution)/shard_map/ppermute | solution.py:251
  48.9 16.8 %collective-permute-start.8 = (bf16[512,192]{0,1:T(8,128)(2,1)}, bf16[512,192]{0,1:T(8,128)(2,1)}, u32[]{:S(2)}, u32[]{:S(2)}) collective-permute-start(bf16[512,192]{0,1:T(8,128)(2,1)} %bitcast.6), channel_id=1, source_target_pairs={{0,7},{1,0},{2,1},{3,2},{4,3},{5,4},{6,5},{7,6},{8,15},{9,8},{10,9... | collective-permute-start | bytes 589832 | tf_op jit(solution)/shard_map/ppermute | solution.py:256
  53.4 6.2 copy-start.22
  54.9 15.5 %collective-permute-start = (bf16[512,192]{0,1:T(8,128)(2,1)}, bf16[512,192]{0,1:T(8,128)(2,1)}, u32[]{:S(2)}, u32[]{:S(2)}) collective-permute-start(bf16[512,192]{0,1:T(8,128)(2,1)} %get-tuple-element.997), channel_id=1, source_target_pairs={{0,1},{1,2},{2,3},{3,4},{4,5},{5,6},{6,7},{7,0},{8,9},{9,10},{10,1... | collective-permute-start | bytes 589832 | tf_op jit(solution)/shard_map/ppermute | solution.py:251
  54.9 18.7 %collective-permute-start.1 = (bf16[512,192]{0,1:T(8,128)(2,1)}, bf16[512,192]{0,1:T(8,128)(2,1)}, u32[]{:S(2)}, u32[]{:S(2)}) collective-permute-start(bf16[512,192]{0,1:T(8,128)(2,1)} %get-tuple-element.997), channel_id=1, source_target_pairs={{0,7},{1,0},{2,1},{3,2},{4,3},{5,4},{6,5},{7,6},{8,15},{9,8},{10,9... | collective-permute-start | bytes 589832 | tf_op jit(solution)/shard_map/ppermute | solution.py:256
  65.7 15.9 %collective-permute-start.9 = (bf16[512,192]{0,1:T(8,128)(2,1)}, bf16[512,192]{0,1:T(8,128)(2,1)S(1)}, u32[]{:S(2)}, u32[]{:S(2)}) collective-permute-start(bf16[512,192]{0,1:T(8,128)(2,1)} %collective-permute-done.7), channel_id=1, source_target_pairs={{0,1},{1,2},{2,3},{3,4},{4,5},{5,6},{6,7},{7,0},{8,9},{9,10},{10,1... | collective-permute-start | bytes 589832 | tf_op jit(solution)/shard_map/ppermute | solution.py:251
  65.7 15.9 %collective-permute-start.10 = (bf16[512,192]{0,1:T(8,128)(2,1)}, bf16[512,192]{0,1:T(8,128)(2,1)S(1)}, u32[]{:S(2)}, u32[]{:S(2)}) collective-permute-start(bf16[512,192]{0,1:T(8,128)(2,1)} %collective-permute-done.8), channel_id=1, source_target_pairs={{0,7},{1,0},{2,1},{3,2},{4,3},{5,4},{6,5},{7,6},{8,15},{9,8},{10,9... | collective-permute-start | bytes 589832 | tf_op jit(solution)/shard_map/ppermute | solution.py:256
  70.4 15.9 %collective-permute-start.2 = (bf16[512,192]{0,1:T(8,128)(2,1)}, bf16[512,192]{0,1:T(8,128)(2,1)S(1)}, u32[]{:S(2)}, u32[]{:S(2)}) collective-permute-start(bf16[512,192]{0,1:T(8,128)(2,1)} %collective-permute-done), channel_id=1, source_target_pairs={{0,1},{1,2},{2,3},{3,4},{4,5},{5,6},{6,7},{7,0},{8,9},{9,10},{10,1... | collective-permute-start | bytes 589832 | tf_op jit(solution)/shard_map/ppermute | solution.py:251
  73.7 16.1 %collective-permute-start.3 = (bf16[512,192]{0,1:T(8,128)(2,1)}, bf16[512,192]{0,1:T(8,128)(2,1)S(1)}, u32[]{:S(2)}, u32[]{:S(2)}) collective-permute-start(bf16[512,192]{0,1:T(8,128)(2,1)} %collective-permute-done.1), channel_id=1, source_target_pairs={{0,7},{1,0},{2,1},{3,2},{4,3},{5,4},{6,5},{7,6},{8,15},{9,8},{10,9... | collective-permute-start | bytes 589832 | tf_op jit(solution)/shard_map/ppermute | solution.py:256
  81.6 12.6 %collective-permute-start.11 = (bf16[512,192]{0,1:T(8,128)(2,1)S(1)}, bf16[512,192]{0,1:T(8,128)(2,1)S(1)}, u32[]{:S(2)}, u32[]{:S(2)}) collective-permute-start(bf16[512,192]{0,1:T(8,128)(2,1)S(1)} %collective-permute-done.9), channel_id=1, source_target_pairs={{0,1},{1,2},{2,3},{3,4},{4,5},{5,6},{6,7},{7,0},{8,9},{9,10},{10,1... | collective-permute-start | bytes 589832 | tf_op jit(solution)/shard_map/ppermute | solution.py:251
  81.6 21.3 %collective-permute-start.12 = (bf16[512,192]{0,1:T(8,128)(2,1)S(1)}, bf16[512,192]{0,1:T(8,128)(2,1)S(1)}, u32[]{:S(2)}, u32[]{:S(2)}) collective-permute-start(bf16[512,192]{0,1:T(8,128)(2,1)S(1)} %collective-permute-done.10), channel_id=1, source_target_pairs={{0,7},{1,0},{2,1},{3,2},{4,3},{5,4},{6,5},{7,6},{8,15},{9,8},{10,9... | collective-permute-start | bytes 589832 | tf_op jit(solution)/shard_map/ppermute | solution.py:256
  86.3 12.2 %collective-permute-start.4 = (bf16[512,192]{0,1:T(8,128)(2,1)S(1)}, bf16[512,192]{0,1:T(8,128)(2,1)S(1)}, u32[]{:S(2)}, u32[]{:S(2)}) collective-permute-start(bf16[512,192]{0,1:T(8,128)(2,1)S(1)} %collective-permute-done.2), channel_id=1, source_target_pairs={{0,1},{1,2},{2,3},{3,4},{4,5},{5,6},{6,7},{7,0},{8,9},{9,10},{10,1... | collective-permute-start | bytes 589832 | tf_op jit(solution)/shard_map/ppermute | solution.py:251
  89.8 15.6 %collective-permute-start.5 = (bf16[512,192]{0,1:T(8,128)(2,1)S(1)}, bf16[512,192]{0,1:T(8,128)(2,1)S(1)}, u32[]{:S(2)}, u32[]{:S(2)}) collective-permute-start(bf16[512,192]{0,1:T(8,128)(2,1)S(1)} %collective-permute-done.3), channel_id=1, source_target_pairs={{0,7},{1,0},{2,1},{3,2},{4,3},{5,4},{6,5},{7,6},{8,15},{9,8},{10,9... | collective-permute-start | bytes 589832 | tf_op jit(solution)/shard_map/ppermute | solution.py:256
  94.2 11.8 %collective-permute-start.13 = (bf16[512,192]{0,1:T(8,128)(2,1)S(1)}, bf16[512,192]{0,1:T(8,128)(2,1)S(1)}, u32[]{:S(2)}, u32[]{:S(2)}) collective-permute-start(bf16[512,192]{0,1:T(8,128)(2,1)S(1)} %collective-permute-done.11), channel_id=1, source_target_pairs={{0,1},{1,2},{2,3},{3,4},{4,5},{5,6},{6,7},{7,0},{8,9},{9,10},{10,1... | collective-permute-start | bytes 589832 | tf_op jit(solution)/shard_map/ppermute | solution.py:251
  98.6 9.5 collective-permute-start.6
  120.1 4.7 copy-start.3
  130.3 4.7 copy-start.3
  168.3 50.7 %all-gather.8.cloned.1.call-start = ((), (), s32[]{:S(2)}) async-start(), calls=%async_computation.8 | async-start | bytes 1966080 | tf_op jit(solution)/shard_map/all_gather | solution.py:184
  199.1 40.9 %all-gather.10.cloned.1.call-start = ((), (), s32[]{:S(2)}) async-start(), calls=%async_computation.10 | async-start | bytes 1966080 | tf_op jit(solution)/shard_map/all_gather | solution.py:184
  199.7 80.4 %reduce-scatter.11.cloned.1.call-start = ((), (), s32[]{:S(2)}) async-start(), calls=%async_computation.11 | async-start | bytes 1966080 | tf_op jit(solution)/shard_map/reduce_scatter | solution.py:188
  218.9 5.7 copy-start.55
  218.9 5.7 copy-start.57
  240.1 6.3 copy-start.54
  252.0 53.2 %all-gather.12.cloned.1.call-start = ((), (), s32[]{:S(2)}) async-start(), calls=%async_computation.12 | async-start | bytes 1966080 | tf_op jit(solution)/shard_map/all_gather | solution.py:184
  285.4 145.7 %reduce-scatter.13.cloned.1.call-start = ((), (), s32[]{:S(2)}) async-start(), calls=%async_computation.13 | async-start | bytes 1769472 | tf_op jit(solution)/shard_map/reduce_scatter | solution.py:266
  332.3 6.8 copy-start.2
  346.7 6.9 copy-start.2
  364.8 135.2 %reduce-scatter.15.cloned.1.call-start = ((), (), s32[]{:S(2)}) async-start(), calls=%async_computation.14 | async-start | bytes 1769472 | tf_op jit(solution)/shard_map/reduce_scatter | solution.py:266
  374.2 5.0 copy-start.15
  374.2 5.0 copy-start.17
  374.2 158.3 %reduce-scatter.17.cloned.1.call-start = ((), (), s32[]{:S(2)}) async-start(), calls=%async_computation.15 | async-start | bytes 1966080 | tf_op jit(solution)/shard_map/reduce_scatter | solution.py:188
  504.0 74.2 %reduce-scatter.9.cloned.1.call-start = ((), (), s32[]{:S(2)}) async-start(), calls=%async_computation.9 | async-start | bytes 1966080 | tf_op jit(solution)/shard_map/reduce_scatter | solution.py:188
  508.2 465.2 %all-reduce.3.cloned.1.call-start = ((), (), s32[]{:S(2)}) async-start(), calls=%async_computation.16 | async-start | bytes 25952256 | tf_op jit(solution)/shard_map/psum | solution.py:336
  508.5 5.6 copy-start.58
  508.5 5.6 copy-start.62
  528.5 49.7 %copy-start.4 = (bf16[128,1536]{1,0:T(8,128)(2,1)S(1)}, bf16[128,1536]{1,0:T(8,128)(2,1)}, u32[]{:S(2)}) copy-start(bf16[128,1536]{1,0:T(8,128)(2,1)} %param.20) | copy-start | bytes 1179652
  528.5 49.7 %copy-start.40 = (f32[1536]{0:T(1024)S(1)}, f32[1536]{0:T(1024)}, u32[]{:S(2)}) copy-start(f32[1536]{0:T(1024)} %convert_element_type.171) | copy-start | bytes 18436
  (63 other events, 157.3 us)
Sparse Core Ops, SparseCore 0:
  9.6 22.3 all-gather.5
  168.4 26.7 reduce-scatter.6
  199.3 19.6 all-gather.7
  220.3 19.6 all-gather.9
  252.1 27.9 reduce-scatter.10
  285.5 19.6 all-gather.11
  365.0 66.0 reduce-scatter.12
  435.1 64.9 reduce-scatter.14
  504.1 26.8 reduce-scatter.16
  533.9 27.9 reduce-scatter.8
  568.8 404.5 all-reduce.2
